TPU v7x, 256 devices: a whole 4x4x8 slice. The times are simulated.
256 devices in a mesh: dp: 8 (over z), vocab: 32 (over x, y, core).
Axes of the slice: x: 4, y: 4, z: 8, core: 2. Of those that a mesh axis runs over, the one named last changes fastest.
Arguments:
- token_ids: int32 [65536], P(('dp', 'vocab')), may hold values from 0 to 152063, as said below
- token_count: int32 [256], P(('dp', 'vocab')), may hold values from 16 to 256
- out_grads: bfloat16 [65536, 5120], P(('dp', 'vocab')), may hold values from -18 to 18
- master_rows: float32 [16384, 5120], P('vocab', 'dp'), may hold values from -0.8 to 0.8
- first_moment: float32 [16384, 5120], P('vocab', 'dp'), may hold values from -4 to 4
- second_moment: float32 [16384, 5120], P('vocab', 'dp'), may hold values from 0.001 to 1
Outputs:
- new_master: float32 [16384, 5120], P('vocab', 'dp')
- new_first: float32 [16384, 5120], P('vocab', 'dp')
- new_second: float32 [16384, 5120], P('vocab', 'dp')
- table_rows: bfloat16 [16384, 5120], P('vocab')
Inputs may be any that keep to these rules, and one draw needn't show every extreme that they name: `token_ids`: within each block of 256 slots, among the live slots (the first token_count of the block) at most 8 have ids in the new rows j * 512 + 135680 to (j + 1) * 512 + 135679 for any one j, and for some j exactly 8 in every block. Slots past token_count hold ids of new rows that are to be ignored.
All inputs are finite; a program needn't handle non-finite values.
Results may differ from a plain program's by a relative error of at most 0.001.
Values may be sent and summed in bfloat16 or wider, within the bound.
No kernel may reach another device: no remote copies, remote signals or barrier semaphores. Data moves between devices by JAX's collectives and lax.ppermute only.
A program may use at most 64 MiB of HBM per device.

v0:
```python
import jax
import jax.numpy as jnp
from jax import lax
from jax.sharding import PartitionSpec as P

VOCAB = 152064
CAP = 8
beta_one = 0.9
beta_two = 0.999
corr_one = 1.0 - 0.9**10
corr_two = 1.0 - 0.999**10
learn_rate = 0.01
epsilon = 1e-08


def body(token_ids, token_count, out_grads, master_rows, first_moment, second_moment):
    owners = lax.axis_size("vocab")
    groups = lax.axis_size("dp")
    rows_own = master_rows.shape[0]
    tok_slots = token_ids.shape[0]
    first_new = VOCAB - rows_own * owners
    position = jnp.arange(tok_slots)
    is_live = (position < token_count[0]) & (token_ids >= first_new)
    new_index = token_ids - first_new
    owner_of = new_index // rows_own
    row_in_owner = new_index % rows_own
    belongs = (owner_of[:, None] == jnp.arange(owners)[None, :]) & is_live[:, None]
    ranking = jnp.cumsum(belongs.astype(jnp.int32), axis=0) - 1
    my_rank = jnp.sum(jnp.where(belongs, ranking, 0), axis=1)
    slot_index = jnp.where(is_live, owner_of * CAP + my_rank, -1)
    placing = jnp.arange(owners * CAP)[:, None] == slot_index[None, :]
    outgoing = jnp.dot(
        placing.astype(jnp.bfloat16), out_grads, preferred_element_type=jnp.float32
    ).astype(jnp.bfloat16)
    slot_row = jnp.max(jnp.where(placing, row_in_owner[None, :], -1), axis=1)
    upper_part = jnp.where(slot_row >= 0, slot_row // 16, -1)
    lower_part = jnp.where(slot_row >= 0, slot_row % 16, 0)
    row_pairs = jnp.stack([upper_part, lower_part], axis=1).astype(jnp.bfloat16)
    tiled_pairs = jnp.tile(row_pairs, (1, groups))
    split_grads, split_pairs = (
        lax.all_to_all(outgoing, "dp", split_axis=1, concat_axis=0, tiled=True),
        lax.all_to_all(tiled_pairs, "dp", split_axis=1, concat_axis=0, tiled=True),
    )
    split_grads = split_grads.reshape(groups, owners * CAP, split_grads.shape[1])
    split_pairs = split_pairs.reshape(groups, owners * CAP, 2)
    arrived, arrived_pairs = (
        lax.all_to_all(split_grads, "vocab", split_axis=1, concat_axis=0, tiled=True),
        lax.all_to_all(split_pairs, "vocab", split_axis=1, concat_axis=0, tiled=True),
    )
    arrived = arrived.reshape(-1, arrived.shape[2])
    arrived_pairs = arrived_pairs.reshape(-1, 2).astype(jnp.float32)
    decoded = arrived_pairs[:, 0] * 16.0 + arrived_pairs[:, 1]
    selector = decoded[None, :] == jnp.arange(rows_own, dtype=jnp.float32)[:, None]
    gradient = jnp.dot(selector.astype(jnp.bfloat16), arrived, preferred_element_type=jnp.float32)
    new_first = beta_one * first_moment + (1.0 - beta_one) * gradient
    new_second = beta_two * second_moment + (1.0 - beta_two) * gradient * gradient
    update = new_first / corr_one / (jnp.sqrt(new_second / corr_two) + epsilon)
    new_master = master_rows - learn_rate * update
    table_rows = lax.all_gather(new_master.astype(jnp.bfloat16), "dp", axis=1, tiled=True)
    return (new_master, new_first, new_second, table_rows)


def solution(mesh):
    return jax.shard_map(
        body,
        mesh=mesh,
        in_specs=(
            P(("dp", "vocab")),
            P(("dp", "vocab")),
            P(("dp", "vocab"), None),
            P("vocab", "dp"),
            P("vocab", "dp"),
            P("vocab", "dp"),
        ),
        out_specs=(P("vocab", "dp"), P("vocab", "dp"), P("vocab", "dp"), P("vocab", None)),
        check_vma=False,
    )
```

profile of v0, /device:TPU:1, one launch (start us, length us, event | category | flops | bytes accessed | tf_op | source)
XLA Modules:
  0.0 226.1 jit_solution(13173120727746846813)
XLA Ops:
  7.2 0.0 copy-start
  8.0 0.7 and_select_fusion.2
  8.7 0.7 fusion.15
  9.4 0.7 compare_and_fusion
  10.0 0.6 reduce-window.6
  10.6 0.2 slice_reduce_fusion
  10.9 0.1 fusion.5
  11.0 0.7 add_select_fusion
  11.7 0.1 select_reduce_fusion
  11.8 0.6 tile.2
  12.4 9.0 %all-to-all-start = ((bf16[256,8,2]{0,2,1:T(2,128)(2,1)}), bf16[256,8,2]{0,2,1:T(2,128)(2,1)S(1)}, u32[]{:S(2)}, u32[]{:S(2)}) async-start(bf16[256,8,2]{0,2,1:T(2,128)(2,1)} %tile.2), calls=%async_computation | async-start | bytes 16384 | tf_op jit(solution)/shard_map/all_to_all | solution.py:42
  21.4 0.0 copy-done
  21.4 0.8 convolution_convert_fusion
  22.3 1.7 copy.51
  24.0 4.0 %all-to-all-done = bf16[256,8,2]{0,2,1:T(2,128)(2,1)S(1)} async-done(((bf16[256,8,2]{0,2,1:T(2,128)(2,1)}), bf16[256,8,2]{0,2,1:T(2,128)(2,1)S(1)}, u32[]{:S(2)}, u32[]{:S(2)}) %all-to-all-start) | async-done | bytes 8224 | tf_op jit(solution)/shard_map/all_to_all | solution.py:42
  28.0 4.4 %all-to-all-start.2 = ((bf16[256,8,640]{2,0,1:T(8,128)(2,1)}), bf16[256,8,640]{2,0,1:T(8,128)(2,1)}, u32[]{:S(2)}, u32[]{:S(2)}) async-start(bf16[256,8,640]{2,0,1:T(8,128)(2,1)} %bitcast.43), calls=%async_computation.2 | async-start | bytes 5242880 | tf_op jit(solution)/shard_map/all_to_all | solution.py:41
  32.4 0.8 copy.39
  33.2 58.8 %all-to-all-done.2 = bf16[256,8,640]{2,0,1:T(8,128)(2,1)} async-done(((bf16[256,8,640]{2,0,1:T(8,128)(2,1)}), bf16[256,8,640]{2,0,1:T(8,128)(2,1)}, u32[]{:S(2)}, u32[]{:S(2)}) %all-to-all-start.2) | async-done | bytes 2621472 | tf_op jit(solution)/shard_map/all_to_all | solution.py:41
  92.0 10.9 %all-to-all-start.1 = ((bf16[8,256,2]{0,2,1:T(2,128)(2,1)}), bf16[8,256,2]{0,2,1:T(2,128)(2,1)S(1)}, u32[]{:S(2)}, u32[]{:S(2)}) async-start(bf16[8,256,2]{0,2,1:T(2,128)(2,1)} %copy.39), calls=%async_computation.1 | async-start | bytes 262144 | tf_op jit(solution)/shard_map/all_to_all | solution.py:48
  103.0 4.7 %copy.43 = bf16[8,256,640]{2,0,1:T(8,128)(2,1)} copy(bf16[8,256,640]{2,1,0:T(8,128)(2,1)} %bitcast.8) | data formatting | bytes 5242880 | tf_op jit(solution)/shard_map/all_to_all | solution.py:41
  107.7 2.9 %all-to-all-done.1 = bf16[8,256,2]{0,2,1:T(2,128)(2,1)S(1)} async-done(((bf16[8,256,2]{0,2,1:T(2,128)(2,1)}), bf16[8,256,2]{0,2,1:T(2,128)(2,1)S(1)}, u32[]{:S(2)}, u32[]{:S(2)}) %all-to-all-start.1) | async-done | bytes 8224 | tf_op jit(solution)/shard_map/all_to_all | solution.py:48
  110.7 4.8 %all-to-all-start.3 = ((bf16[8,256,640]{2,0,1:T(8,128)(2,1)}), bf16[8,256,640]{2,0,1:T(8,128)(2,1)}, u32[]{:S(2)}, u32[]{:S(2)}) async-start(bf16[8,256,640]{2,0,1:T(8,128)(2,1)} %copy.43), calls=%async_computation.3 | async-start | bytes 5242880 | tf_op jit(solution)/shard_map/all_to_all | solution.py:47
  115.4 0.0 all-gather.2.cloned.1.call-start
  115.5 0.1 copy.40
  115.6 0.2 reshape.169
  115.8 0.2 copy.41
  115.9 0.2 reshape.168
  116.1 33.4 %all-to-all-done.3 = bf16[8,256,640]{2,0,1:T(8,128)(2,1)} async-done(((bf16[8,256,640]{2,0,1:T(8,128)(2,1)}), bf16[8,256,640]{2,0,1:T(8,128)(2,1)}, u32[]{:S(2)}, u32[]{:S(2)}) %all-to-all-start.3) | async-done | bytes 2621472 | tf_op jit(solution)/shard_map/all_to_all | solution.py:47
  149.5 0.0 copy-start.1
  149.5 0.0 copy-start.2
  149.5 0.0 copy-start.3
  149.5 2.4 %copy.45 = bf16[32,8,8,640]{3,2,1,0:T(8,128)(2,1)S(1)} copy(bf16[32,8,8,640]{3,1,2,0:T(8,128)(2,1)} %bitcast.11) | data formatting | bytes 5242880 | tf_op jit(solution)/shard_map/all_to_all | solution.py:47
  151.9 0.0 copy-done.1
  151.9 0.1 copy-done.2
  152.0 0.4 copy-done.3
  152.4 4.7 %fusion.11 = (bf16[512,640]{1,0:T(8,128)(2,1)}, f32[512,640]{1,0:T(8,128)}, f32[512,640]{1,0:T(8,128)}, f32[512,640]{1,0:T(8,128)}) fusion(f32[512,640]{1,0:T(8,128)S(1)} %copy-done.1, f32[512,640]{1,0:T(8,128)S(1)} %copy-done.2, f32[512,640]{1,0:T(8,128)S(1)} %copy-done.3, bf16[2048,640]{1,0:T(8,128)(2,1)S(1)} %bitcast.45, f32[2048]{0:T(1024)S(1)} %bitcast.49), kind=kOutput, calls=%fused_computation.43 | convolution fusion | flops 1347813376 | bytes 11149312 | tf_op jit(solution)/shard_map/dot_general | solution.py:54
  157.1 0.0 all-gather.2.cloned.1.call-update
  157.1 57.0 %all-gather.2.cloned.1.call-done = bf16[512,5120]{1,0:T(8,128)(2,1)} async-done(((bf16[512,640]{1,0:T(8,128)(2,1)}), bf16[512,5120]{1,0:T(8,128)(2,1)}) %all-gather.2.cloned.1.call-update) | async-done | bytes 5242896 | tf_op jit(solution)/shard_map/all_gather | solution.py:59
  214.1 5.2 %copy.54 = bf16[512,5120]{1,0:T(8,128)(2,1)} copy(bf16[512,5120]{1,0:T(8,128)(2,1)} %all-gather.2.cloned.1.call-done) | data formatting | bytes 10485760
  (6 shorter events, 0.1 us)
Async XLA Ops:
  7.2 14.3 %copy-start = (bf16[256,5120]{1,0:T(8,128)(2,1)S(1)}, bf16[256,5120]{1,0:T(8,128)(2,1)}, u32[]{:S(2)}) copy-start(bf16[256,5120]{1,0:T(8,128)(2,1)} %param.8) | copy-start | bytes 7864324
  12.4 15.6 %all-to-all-start = ((bf16[256,8,2]{0,2,1:T(2,128)(2,1)}), bf16[256,8,2]{0,2,1:T(2,128)(2,1)S(1)}, u32[]{:S(2)}, u32[]{:S(2)}) async-start(bf16[256,8,2]{0,2,1:T(2,128)(2,1)} %tile.2), calls=%async_computation | async-start | bytes 16384 | tf_op jit(solution)/shard_map/all_to_all | solution.py:42
  28.0 64.0 %all-to-all-start.2 = ((bf16[256,8,640]{2,0,1:T(8,128)(2,1)}), bf16[256,8,640]{2,0,1:T(8,128)(2,1)}, u32[]{:S(2)}, u32[]{:S(2)}) async-start(bf16[256,8,640]{2,0,1:T(8,128)(2,1)} %bitcast.43), calls=%async_computation.2 | async-start | bytes 5242880 | tf_op jit(solution)/shard_map/all_to_all | solution.py:41
  92.0 18.6 %all-to-all-start.1 = ((bf16[8,256,2]{0,2,1:T(2,128)(2,1)}), bf16[8,256,2]{0,2,1:T(2,128)(2,1)S(1)}, u32[]{:S(2)}, u32[]{:S(2)}) async-start(bf16[8,256,2]{0,2,1:T(2,128)(2,1)} %copy.39), calls=%async_computation.1 | async-start | bytes 262144 | tf_op jit(solution)/shard_map/all_to_all | solution.py:48
  110.7 38.9 %all-to-all-start.3 = ((bf16[8,256,640]{2,0,1:T(8,128)(2,1)}), bf16[8,256,640]{2,0,1:T(8,128)(2,1)}, u32[]{:S(2)}, u32[]{:S(2)}) async-start(bf16[8,256,640]{2,0,1:T(8,128)(2,1)} %copy.43), calls=%async_computation.3 | async-start | bytes 5242880 | tf_op jit(solution)/shard_map/all_to_all | solution.py:47
  115.4 98.7 %all-gather.2.cloned.1.call-start = ((), (), s32[]{:S(2)}) async-start(), calls=%async_computation.4 | async-start | bytes 5898240 | tf_op jit(solution)/shard_map/all_gather | solution.py:59
  149.5 2.4 %copy-start.1 = (f32[512,640]{1,0:T(8,128)S(1)}, f32[512,640]{1,0:T(8,128)}, u32[]{:S(2)}) copy-start(f32[512,640]{1,0:T(8,128)} %param.9) | copy-start | bytes 3932164
  149.5 2.5 %copy-start.2 = (f32[512,640]{1,0:T(8,128)S(1)}, f32[512,640]{1,0:T(8,128)}, u32[]{:S(2)}) copy-start(f32[512,640]{1,0:T(8,128)} %param.10) | copy-start | bytes 3932164
  149.5 2.9 %copy-start.3 = (f32[512,640]{1,0:T(8,128)S(1)}, f32[512,640]{1,0:T(8,128)}, u32[]{:S(2)}) copy-start(f32[512,640]{1,0:T(8,128)} %param.11) | copy-start | bytes 3932164
Sparse Core Ops, SparseCore 0:
  157.2 56.8 all-gather.1
where the time goes:
time: 227 us; the launch traced here: 226 us
  waiting for transfers between devices  156 us (69%)
  starting transfers between devices  29.2 us (13%)
  local copies, waits for them, and re-layouts  16.7 us (7%)
  between operations  14.9 us (7%)
  matrix products  5.52 us (2%)
  other arithmetic  3.65 us (2%)
    all_to_all x1, waiting for transfers between devices, body(): lax.all_to_all(outgoing, 'dp', split_axis=1, concat_axis=0, tiled=True)  58.8 us
    all_gather x1, waiting for transfers between devices, body(): lax.all_gather(new_master.astype(jnp.bfloat16), 'dp', axis=1, tiled=True)  57 us
    all_to_all x1, waiting for transfers between devices, body(): lax.all_to_all(split_grads, 'vocab', split_axis=1, concat_axis=0, tiled=T...  33.4 us
    all_to_all x1, starting transfers between devices, body(): lax.all_to_all(split_pairs, 'vocab', split_axis=1, concat_axis=0, tiled=T...  10.9 us
    all_to_all x1, starting transfers between devices, body(): lax.all_to_all(tiled_pairs, 'dp', split_axis=1, concat_axis=0, tiled=True)  9 us
    all_to_all x2, local copies, waits for them, and re-layouts, body(): lax.all_to_all(outgoing, 'dp', split_axis=1, concat_axis=0, tiled=True)  6.47 us
    unnamed x9, local copies, waits for them, and re-layouts  5.69 us
    all_to_all x1, starting transfers between devices, body(): lax.all_to_all(split_grads, 'vocab', split_axis=1, concat_axis=0, tiled=T...  4.79 us
  transfers between devices with their start and end apart: 5, of which 5 were waited for; matrix products, arithmetic and copies ran while one was open for 4% of the time, Pallas kernels for 0%

commit v1 on v0

--- a/solution.py
+++ b/solution.py
@@ -11,6 +11,29 @@
 corr_two = 1.0 - 0.999**10
 learn_rate = 0.01
 epsilon = 1e-08
+
+
+def split_up(shard, dim, size):
+    lengths = shard.shape
+    blocks = shard.reshape(*lengths[:dim], size, lengths[dim] // size, *lengths[dim + 1 :])
+    return jnp.moveaxis(blocks, dim, 0)
+
+
+def in_order(tiles, dim):
+    tiles = jnp.moveaxis(tiles, 0, dim)
+    lengths = tiles.shape
+    return tiles.reshape(*lengths[:dim], lengths[dim] * lengths[dim + 1], *lengths[dim + 2 :])
+
+
+def rotated_exchange(value, axis, split_dim, concat_dim):
+    count, index = (lax.axis_size(axis), lax.axis_index(axis))
+    blocks = split_up(value, split_dim, count)
+    done = [blocks[index]]
+    for step in range(1, count):
+        sent = blocks[(index + step) % count]
+        done.append(lax.ppermute(sent, axis, [(i, (i + step) % count) for i in range(count)]))
+    blocks = jnp.stack(done)[(index - jnp.arange(count)) % count]
+    return in_order(blocks, concat_dim)
 
 
 def body(token_ids, token_count, out_grads, master_rows, first_moment, second_moment):
@@ -38,7 +61,7 @@
     row_pairs = jnp.stack([upper_part, lower_part], axis=1).astype(jnp.bfloat16)
     tiled_pairs = jnp.tile(row_pairs, (1, groups))
     split_grads, split_pairs = (
-        lax.all_to_all(outgoing, "dp", split_axis=1, concat_axis=0, tiled=True),
+        rotated_exchange(outgoing, "dp", 1, 0),
         lax.all_to_all(tiled_pairs, "dp", split_axis=1, concat_axis=0, tiled=True),
     )
     split_grads = split_grads.reshape(groups, owners * CAP, split_grads.shape[1])

time: 227 us -> 239 us (1.053)
  waiting for transfers between devices: 156 us -> 122 us
  local copies, waits for them, and re-layouts: 16.7 us -> 50 us
  starting transfers between devices: 29.2 us -> 42.3 us
    all_to_all x1 -> x0, waiting for transfers between devices: 58.8 us -> none  [body(): lax.all_to_all(outgoing, 'dp', split_axis=1, concat_axis=0, tiled=True)]
    ppermute x0 -> x7, waiting for transfers between devices: none -> 29.8 us  [rotated_exchange(): lax.ppermute(sent, axis, [(i, (i + step) % count) for i in range(count)])]
    unnamed x9 -> x24, local copies, waits for them, and re-layouts: 5.69 us -> 21.3 us
    another operation x1 -> x3, local copies, waits for them, and re-layouts: 0.01 us -> 15.4 us
    ppermute x0 -> x7, starting transfers between devices: none -> 15 us  [rotated_exchange(): lax.ppermute(sent, axis, [(i, (i + step) % count) for i in range(count)])]
    gather x0 -> x2, local copies, waits for them, and re-layouts: none -> 8.84 us  [rotated_exchange(): blocks = jnp.stack(done)[(index - jnp.arange(count)) % count]]
    all_to_all x2 -> x0, local copies, waits for them, and re-layouts: 6.47 us -> none  [body(): lax.all_to_all(outgoing, 'dp', split_axis=1, concat_axis=0, tiled=True)]
    all_to_all x1 -> x0, starting transfers between devices: 4.39 us -> none  [body(): lax.all_to_all(outgoing, 'dp', split_axis=1, concat_axis=0, tiled=True)]
  transfers between devices with their start and end apart: 5 -> 11, of which waited for: 5 -> 6; matrix products, arithmetic and copies ran while one was open for 4% -> 18% of each run, Pallas kernels for 0% -> 0%
where the time goes in v1:
time: 239 us
  waiting for transfers between devices  122 us (51%)
  local copies, waits for them, and re-layouts  50 us (21%)
  starting transfers between devices  42.3 us (18%)
  between operations  15 us (6%)
  matrix products  5.52 us (2%)
  other arithmetic  3.66 us (2%)
    all_gather x1, waiting for transfers between devices, body(): lax.all_gather(new_master.astype(jnp.bfloat16), 'dp', axis=1, tiled=True)  59.3 us
    all_to_all x1, waiting for transfers between devices, body(): lax.all_to_all(split_grads, 'vocab', split_axis=1, concat_axis=0, tiled=T...  33.3 us
    ppermute x7, waiting for transfers between devices, rotated_exchange(): lax.ppermute(sent, axis, [(i, (i + step) % count) for i in range(count)])  29.8 us
    unnamed x24, local copies, waits for them, and re-layouts  21.3 us
    ppermute x7, starting transfers between devices, rotated_exchange(): lax.ppermute(sent, axis, [(i, (i + step) % count) for i in range(count)])  15 us
    another operation x2, local copies, waits for them, and re-layouts  14.6 us
    all_to_all x1, starting transfers between devices, body(): lax.all_to_all(split_pairs, 'vocab', split_axis=1, concat_axis=0, tiled=T...  9.72 us
    all_to_all x1, starting transfers between devices, body(): lax.all_to_all(tiled_pairs, 'dp', split_axis=1, concat_axis=0, tiled=True)  9 us
  transfers between devices with their start and end apart: 11, of which 6 were waited for; matrix products, arithmetic and copies ran while one was open for 18% of the time, Pallas kernels for 0%

profile of v1, /device:TPU:1, one launch (start us, length us, event | category | flops | bytes accessed | tf_op | source)
XLA Modules:
  0.0 238.9 jit_solution(17557561283690275125)
XLA Ops:
  8.0 0.7 and_select_fusion.3
  8.7 0.7 fusion.18
  9.4 0.7 compare_and_fusion
  10.0 0.6 reduce-window.6
  11.0 0.7 add_select_fusion
  11.8 0.6 tile.2
  12.4 9.0 %all-to-all-start = ((bf16[256,8,2]{0,2,1:T(2,128)(2,1)}), bf16[256,8,2]{0,2,1:T(2,128)(2,1)S(1)}, u32[]{:S(2)}, u32[]{:S(2)}) async-start(bf16[256,8,2]{0,2,1:T(2,128)(2,1)} %tile.2), calls=%async_computation | async-start | bytes 16384 | tf_op jit(solution)/shard_map/all_to_all | solution.py:65
  21.4 0.8 convolution_convert_fusion
  22.3 2.0 copy.100
  24.3 14.6 %constant_dynamic-slice_fusion = (bf16[256,1,640]{2,1,0:T(2,128)(2,1)S(1)}, bf16[256,1,640]{2,1,0:T(2,128)(2,1)S(1)}, bf16[256,1,640]{2,1,0:T(2,128)(2,1)S(1)}, ...) fusion(bf16[256,8,640]{2,1,0:T(8,128)(2,1)} %bitcast.81, ...), kind=kLoop, calls=%fused_computation.51 | loop fusion | bytes 5242912 | tf_op jit(solution)/shard_map/dynamic-slice.7
  38.9 0.8 copy.118
  39.7 1.5 collective-permute-start
  41.1 0.8 copy.117
  41.9 2.1 collective-permute-start.1
  44.0 0.8 copy.116
  44.7 2.4 %collective-permute-start.2 = (bf16[256,640]{1,0:T(8,128)(2,1)}, bf16[256,640]{1,0:T(8,128)(2,1)}, u32[]{:S(2)}, u32[]{:S(2)}) collective-permute-start(bf16[256,640]{1,0:T(8,128)(2,1)} %bitcast.75), channel_id=1, source_target_pairs={{0,96},{32,128},{64,160},{96,192},{128,224},{160,0},{192,32},{224,... | collective-permute-start | bytes 983048 | tf_op jit(solution)/shard_map/ppermute | solution.py:34
  47.1 0.8 copy.115
  47.9 2.1 collective-permute-start.3
  50.0 0.8 copy.114
  50.8 2.4 %collective-permute-start.4 = (bf16[256,640]{1,0:T(8,128)(2,1)}, bf16[256,640]{1,0:T(8,128)(2,1)S(1)}, u32[]{:S(2)}, u32[]{:S(2)}) collective-permute-start(bf16[256,640]{1,0:T(8,128)(2,1)} %bitcast.73), channel_id=1, source_target_pairs={{0,160},{32,192},{64,224},{96,0},{128,32},{160,64},{192,96},{224,1... | collective-permute-start | bytes 983048 | tf_op jit(solution)/shard_map/ppermute | solution.py:34
  53.2 0.8 fusion.3
  53.9 0.8 copy.112
  54.7 0.8 copy.113
  55.5 0.8 copy.76
  56.3 9.7 %all-to-all-start.1 = ((bf16[8,256,2]{0,2,1:T(2,128)(2,1)}), bf16[8,256,2]{0,2,1:T(2,128)(2,1)S(1)}, u32[]{:S(2)}, u32[]{:S(2)}) async-start(bf16[8,256,2]{0,2,1:T(2,128)(2,1)} %copy.76), calls=%async_computation.1 | async-start | bytes 262144 | tf_op jit(solution)/shard_map/all_to_all | solution.py:71
  66.1 3.4 %collective-permute-start.5 = (bf16[256,640]{1,0:T(8,128)(2,1)}, bf16[256,640]{1,0:T(8,128)(2,1)S(1)}, u32[]{:S(2)}, u32[]{:S(2)}) collective-permute-start(bf16[256,640]{1,0:T(8,128)(2,1)} %bitcast.86), channel_id=1, source_target_pairs={{0,192},{32,224},{64,0},{96,32},{128,64},{160,96},{192,128},{224,1... | collective-permute-start | bytes 983048 | tf_op jit(solution)/shard_map/ppermute | solution.py:34
  69.4 1.7 bitcast_dynamic-update-slice_fusion.6
  71.2 1.2 collective-permute-start.6
  72.3 1.7 bitcast_dynamic-update-slice_fusion.5
  74.1 3.7 %collective-permute-done.2 = bf16[256,640]{1,0:T(8,128)(2,1)} collective-permute-done((bf16[256,640]{1,0:T(8,128)(2,1)}, bf16[256,640]{1,0:T(8,128)(2,1)}, u32[]{:S(2)}, u32[]{:S(2)}) %collective-permute-start.2) | collective-permute-done | bytes 327712 | tf_op jit(solution)/shard_map/ppermute | solution.py:34
  77.8 1.7 bitcast_dynamic-update-slice_fusion.4
  79.5 14.5 %collective-permute-done.3 = bf16[256,640]{1,0:T(8,128)(2,1)S(1)} collective-permute-done((bf16[256,640]{1,0:T(8,128)(2,1)}, bf16[256,640]{1,0:T(8,128)(2,1)S(1)}, u32[]{:S(2)}, u32[]{:S(2)}) %collective-permute-start.3) | collective-permute-done | bytes 327712 | tf_op jit(solution)/shard_map/ppermute | solution.py:34
  94.0 0.8 bitcast_dynamic-update-slice_fusion.3
  94.8 0.8 bitcast_dynamic-update-slice_fusion.2
  95.5 7.5 %collective-permute-done.5 = bf16[256,640]{1,0:T(8,128)(2,1)S(1)} collective-permute-done((bf16[256,640]{1,0:T(8,128)(2,1)}, bf16[256,640]{1,0:T(8,128)(2,1)S(1)}, u32[]{:S(2)}, u32[]{:S(2)}) %collective-permute-start.5) | collective-permute-done | bytes 327712 | tf_op jit(solution)/shard_map/ppermute | solution.py:34
  103.0 0.8 bitcast_dynamic-update-slice_fusion.1
  103.7 4.1 %collective-permute-done.6 = bf16[256,640]{1,0:T(8,128)(2,1)S(1)} collective-permute-done((bf16[256,640]{1,0:T(8,128)(2,1)}, bf16[256,640]{1,0:T(8,128)(2,1)S(1)}, u32[]{:S(2)}, u32[]{:S(2)}) %collective-permute-start.6) | collective-permute-done | bytes 327712 | tf_op jit(solution)/shard_map/ppermute | solution.py:34
  107.8 0.8 bitcast_dynamic-update-slice_fusion
  108.6 4.1 %gather_fusion = bf16[8,256,640]{2,1,0:T(8,128)(2,1)} fusion(bf16[8,256,640]{2,1,0:T(8,128)(2,1)} %bitcast_dynamic-update-slice_fusion, s32[1024]{0:T(1024)S(1)} %pad_clamp_fusion), kind=kCustom, calls=%fused_computation | custom fusion | bytes 5242912 | tf_op jit(solution)/shard_map/gather | solution.py:35
  112.7 4.7 %copy.87 = bf16[8,256,640]{2,0,1:T(8,128)(2,1)} copy(bf16[8,256,640]{2,1,0:T(8,128)(2,1)} %gather_fusion) | data formatting | bytes 5242880 | tf_op jit(solution)/shard_map/gather | solution.py:35
  117.4 8.6 %all-to-all-start.2 = ((bf16[8,256,640]{2,0,1:T(8,128)(2,1)}), bf16[8,256,640]{2,0,1:T(8,128)(2,1)}, u32[]{:S(2)}, u32[]{:S(2)}) async-start(bf16[8,256,640]{2,0,1:T(8,128)(2,1)} %copy.87), calls=%async_computation.2 | async-start | bytes 5242880 | tf_op jit(solution)/shard_map/all_to_all | solution.py:70
  126.1 0.2 reshape.232
  126.7 33.3 %all-to-all-done.2 = bf16[8,256,640]{2,0,1:T(8,128)(2,1)} async-done(((bf16[8,256,640]{2,0,1:T(8,128)(2,1)}), bf16[8,256,640]{2,0,1:T(8,128)(2,1)}, u32[]{:S(2)}, u32[]{:S(2)}) %all-to-all-start.2) | async-done | bytes 2621472 | tf_op jit(solution)/shard_map/all_to_all | solution.py:70
  160.0 2.4 copy.89
  162.5 0.4 copy-done.3
  162.9 4.7 %fusion.14 = (bf16[512,640]{1,0:T(8,128)(2,1)}, f32[512,640]{1,0:T(8,128)}, f32[512,640]{1,0:T(8,128)}, f32[512,640]{1,0:T(8,128)}) fusion(f32[512,640]{1,0:T(8,128)S(1)} %copy-done.1, f32[512,640]{1,0:T(8,128)S(1)} %copy-done.2, f32[512,640]{1,0:T(8,128)S(1)} %copy-done.3, bf16[2048,640]{1,0:T(8,128)(2,1)S(1)} %bitcast.83, f32[2048]{0:T(1024)S(1)} %bitcast.89), kind=kOutput, calls=%fused_computation.74 | convolution fusion | flops 1347813376 | bytes 11149312 | tf_op jit(solution)/shard_map/dot_general | solution.py:77
  167.6 59.3 %all-gather.2.cloned.1.call-done = bf16[512,5120]{1,0:T(8,128)(2,1)} async-done(((bf16[512,640]{1,0:T(8,128)(2,1)}), bf16[512,5120]{1,0:T(8,128)(2,1)}) %all-gather.2.cloned.1.call-update) | async-done | bytes 5242896 | tf_op jit(solution)/shard_map/all_gather | solution.py:82
  226.9 5.2 %copy.128 = bf16[512,5120]{1,0:T(8,128)(2,1)} copy(bf16[512,5120]{1,0:T(8,128)(2,1)} %all-gather.2.cloned.1.call-done) | data formatting | bytes 10485760
  (28 shorter events, 1.1 us)
Async XLA Ops:
  7.2 14.3 %copy-start = (bf16[256,5120]{1,0:T(8,128)(2,1)S(1)}, bf16[256,5120]{1,0:T(8,128)(2,1)}, u32[]{:S(2)}) copy-start(bf16[256,5120]{1,0:T(8,128)(2,1)} %param.8) | copy-start | bytes 7864324
  12.4 43.1 %all-to-all-start = ((bf16[256,8,2]{0,2,1:T(2,128)(2,1)}), bf16[256,8,2]{0,2,1:T(2,128)(2,1)S(1)}, u32[]{:S(2)}, u32[]{:S(2)}) async-start(bf16[256,8,2]{0,2,1:T(2,128)(2,1)} %tile.2), calls=%async_computation | async-start | bytes 16384 | tf_op jit(solution)/shard_map/all_to_all | solution.py:65
  39.7 26.4 %collective-permute-start = (bf16[256,640]{1,0:T(8,128)(2,1)}, bf16[256,640]{1,0:T(8,128)(2,1)}, u32[]{:S(2)}, u32[]{:S(2)}) collective-permute-start(bf16[256,640]{1,0:T(8,128)(2,1)} %bitcast.77), channel_id=1, source_target_pairs={{0,32},{32,64},{64,96},{96,128},{128,160},{160,192},{192,224},{224... | collective-permute-start | bytes 983048 | tf_op jit(solution)/shard_map/ppermute | solution.py:34
  41.9 29.3 %collective-permute-start.1 = (bf16[256,640]{1,0:T(8,128)(2,1)}, bf16[256,640]{1,0:T(8,128)(2,1)}, u32[]{:S(2)}, u32[]{:S(2)}) collective-permute-start(bf16[256,640]{1,0:T(8,128)(2,1)} %bitcast.76), channel_id=1, source_target_pairs={{0,64},{32,96},{64,128},{96,160},{128,192},{160,224},{192,0},{224,... | collective-permute-start | bytes 983048 | tf_op jit(solution)/shard_map/ppermute | solution.py:34
  44.7 33.0 %collective-permute-start.2 = (bf16[256,640]{1,0:T(8,128)(2,1)}, bf16[256,640]{1,0:T(8,128)(2,1)}, u32[]{:S(2)}, u32[]{:S(2)}) collective-permute-start(bf16[256,640]{1,0:T(8,128)(2,1)} %bitcast.75), channel_id=1, source_target_pairs={{0,96},{32,128},{64,160},{96,192},{128,224},{160,0},{192,32},{224,... | collective-permute-start | bytes 983048 | tf_op jit(solution)/shard_map/ppermute | solution.py:34
  47.9 46.1 %collective-permute-start.3 = (bf16[256,640]{1,0:T(8,128)(2,1)}, bf16[256,640]{1,0:T(8,128)(2,1)S(1)}, u32[]{:S(2)}, u32[]{:S(2)}) collective-permute-start(bf16[256,640]{1,0:T(8,128)(2,1)} %bitcast.74), channel_id=1, source_target_pairs={{0,128},{32,160},{64,192},{96,224},{128,0},{160,32},{192,64},{224,... | collective-permute-start | bytes 983048 | tf_op jit(solution)/shard_map/ppermute | solution.py:34
  50.8 44.0 %collective-permute-start.4 = (bf16[256,640]{1,0:T(8,128)(2,1)}, bf16[256,640]{1,0:T(8,128)(2,1)S(1)}, u32[]{:S(2)}, u32[]{:S(2)}) collective-permute-start(bf16[256,640]{1,0:T(8,128)(2,1)} %bitcast.73), channel_id=1, source_target_pairs={{0,160},{32,192},{64,224},{96,0},{128,32},{160,64},{192,96},{224,1... | collective-permute-start | bytes 983048 | tf_op jit(solution)/shard_map/ppermute | solution.py:34
  56.3 61.1 %all-to-all-start.1 = ((bf16[8,256,2]{0,2,1:T(2,128)(2,1)}), bf16[8,256,2]{0,2,1:T(2,128)(2,1)S(1)}, u32[]{:S(2)}, u32[]{:S(2)}) async-start(bf16[8,256,2]{0,2,1:T(2,128)(2,1)} %copy.76), calls=%async_computation.1 | async-start | bytes 262144 | tf_op jit(solution)/shard_map/all_to_all | solution.py:71
  66.1 36.9 %collective-permute-start.5 = (bf16[256,640]{1,0:T(8,128)(2,1)}, bf16[256,640]{1,0:T(8,128)(2,1)S(1)}, u32[]{:S(2)}, u32[]{:S(2)}) collective-permute-start(bf16[256,640]{1,0:T(8,128)(2,1)} %bitcast.86), channel_id=1, source_target_pairs={{0,192},{32,224},{64,0},{96,32},{128,64},{160,96},{192,128},{224,1... | collective-permute-start | bytes 983048 | tf_op jit(solution)/shard_map/ppermute | solution.py:34
  71.2 36.7 %collective-permute-start.6 = (bf16[256,640]{1,0:T(8,128)(2,1)}, bf16[256,640]{1,0:T(8,128)(2,1)S(1)}, u32[]{:S(2)}, u32[]{:S(2)}) collective-permute-start(bf16[256,640]{1,0:T(8,128)(2,1)} %bitcast.85), channel_id=1, source_target_pairs={{0,224},{32,0},{64,32},{96,64},{128,96},{160,128},{192,160},{224,1... | collective-permute-start | bytes 983048 | tf_op jit(solution)/shard_map/ppermute | solution.py:34
  117.4 42.6 %all-to-all-start.2 = ((bf16[8,256,640]{2,0,1:T(8,128)(2,1)}), bf16[8,256,640]{2,0,1:T(8,128)(2,1)}, u32[]{:S(2)}, u32[]{:S(2)}) async-start(bf16[8,256,640]{2,0,1:T(8,128)(2,1)} %copy.87), calls=%async_computation.2 | async-start | bytes 5242880 | tf_op jit(solution)/shard_map/all_to_all | solution.py:70
  126.0 100.9 %all-gather.2.cloned.1.call-start = ((), (), s32[]{:S(2)}) async-start(), calls=%async_computation.3 | async-start | bytes 5898240 | tf_op jit(solution)/shard_map/all_gather | solution.py:82
  160.0 2.4 copy-start.1
  160.0 2.5 %copy-start.2 = (f32[512,640]{1,0:T(8,128)S(1)}, f32[512,640]{1,0:T(8,128)}, u32[]{:S(2)}) copy-start(f32[512,640]{1,0:T(8,128)} %param.10) | copy-start | bytes 3932164
  160.0 2.9 %copy-start.3 = (f32[512,640]{1,0:T(8,128)S(1)}, f32[512,640]{1,0:T(8,128)}, u32[]{:S(2)}) copy-start(f32[512,640]{1,0:T(8,128)} %param.11) | copy-start | bytes 3932164
Sparse Core Ops, SparseCore 0:
  167.7 59.1 all-gather.1
